TPU v7x, 32 devices: a whole 2x2x4 slice. The times are simulated.
32 devices in a mesh: groups: 2 (over y), ep: 8 (over z, core), tp: 2 (over x).
Axes of the slice: x: 2, y: 2, z: 4, core: 2. Of those that a mesh axis runs over, the one named last changes fastest.
Arguments:
- hidden: bfloat16 [1024, 2880], P(('groups', 'ep')), parts along dimension 0, may hold values from -6 to 6
- route_experts: int32 [1024, 4], P(('groups', 'ep')), parts along dimension 0, may hold values from 0 to 7, all different within a row; in each aligned block of 64 rows (0 to 63, 64 to 127, ...) at most 64 rows name the same one
- route_weight: float32 [1024, 4], P(('groups', 'ep')), parts along dimension 0, may hold values from 0.1 to 0.6
- norm_gain: bfloat16 [2880], replicated, may hold values from 0.099609375 to 1.8984375
- gate_up_codes: int32 [8, 360, 5120], P('ep', None, 'tp'), may hold values from -2147483648 to 2147483646
- gate_up_scales: bfloat16 [8, 90, 5120], P('ep', None, 'tp'), as said below
- gate_up_bias: bfloat16 [8, 5120], P('ep', 'tp'), may hold values from -3 to 3
- down_codes: int32 [8, 2560, 360], P('ep', 'tp'), may hold values from -2147483648 to 2147483646
- down_scales: bfloat16 [8, 80, 2880], P('ep', 'tp'), as said below
- down_bias: bfloat16 [8, 2880], P('ep', 'tp'), may hold values from -3 to 3
Outputs:
- layer_out: bfloat16 [1024, 2880], P(('groups', 'ep'), 'tp'), parts along dimension 0
There are 2 independent parts, one for each index of `groups`. A program takes and returns all parts, laid end to end along the dimension named above; an argument that names none is the same for every part. Nothing has to cross between parts.
Inputs may be any that keep to these rules, and one draw needn't show every extreme that they name: `route_experts`: each row names 4 different experts. In each aligned block of 64 rows no expert is named by more than 64 rows, and in some blocks one expert is named by exactly 64 rows. `gate_up_scales`: every scale is a power of two. `down_scales`: every scale is a power of two.
All inputs are finite; a program needn't handle non-finite values.
Results may differ from a plain program's by a relative error of at most 0.013.
Values may be sent and summed in bfloat16 or wider, within the bound.
A program may use at most 128 MiB of HBM per device.

v0:
```python
import jax
import jax.numpy as jnp
from jax import lax
from jax.sharding import PartitionSpec as P


def decode_nibble(nibble):
    magnit = nibble & 7
    exponent = jnp.maximum(jnp.right_shift(magnit, 1) - 1, 0)
    doubled = jnp.where(magnit < 2, magnit, jnp.left_shift(2 + (magnit & 1), exponent))
    signed_val = doubled.astype(jnp.float32) * 0.5
    return jnp.where(nibble >= 8, -signed_val, signed_val)


def unpack_weights(packed, scaling):
    row_count = packed.shape[0]
    shifts = jnp.arange(8, dtype=jnp.int32) * 4
    nibble = jnp.right_shift(packed[:, :, None], shifts[None, None, :]) & 15
    nibble = nibble.reshape(row_count, packed.shape[1] * 8)
    signed_val = decode_nibble(nibble)
    signed_val = (
        signed_val.reshape(row_count // 32, 32, -1) * scaling.astype(jnp.float32)[:, None, :]
    )
    return signed_val.reshape(row_count, -1).astype(jnp.bfloat16)


def unpack_rows(packed, scaling):
    row_count = packed.shape[0] * 8
    shifts = jnp.arange(8, dtype=jnp.int32) * 4
    nibble = jnp.right_shift(packed[:, None, :], shifts[None, :, None]) & 15
    nibble = nibble.reshape(row_count, packed.shape[1])
    signed_val = decode_nibble(nibble)
    signed_val = (
        signed_val.reshape(row_count // 32, 32, -1) * scaling.astype(jnp.float32)[:, None, :]
    )
    return signed_val.reshape(row_count, -1).astype(jnp.bfloat16)


def rms_normed(hidden, norm_gain):
    widened = hidden.astype(jnp.float32)
    mean_square = jnp.mean(widened * widened, axis=-1, keepdims=True)
    scaled = widened * lax.rsqrt(mean_square + 1e-05) * norm_gain.astype(jnp.float32)
    return scaled.astype(jnp.bfloat16)


def shards(
    hidden,
    route_experts,
    route_weight,
    norm_gain,
    gate_up_codes,
    gate_up_scales,
    gate_up_bias,
    down_codes,
    down_scales,
    down_bias,
):
    ep_count = lax.axis_size("ep")
    tp_count = lax.axis_size("tp")
    tp_rank = lax.axis_index("tp")
    tok_count, model_width = hidden.shape
    top_count = route_experts.shape[1]
    capacity = min(tok_count, max(tp_count, 2 * tok_count * top_count // ep_count))
    normed = rms_normed(hidden, norm_gain)
    flat_routes = route_experts.reshape(-1)
    onehot = (flat_routes[:, None] == jnp.arange(ep_count, dtype=jnp.int32)[None, :]).astype(
        jnp.int32
    )
    before = jnp.cumsum(onehot, axis=0) - onehot
    slot_of = jnp.sum(before * onehot, axis=1)
    target = (flat_routes * capacity + slot_of).reshape(tok_count, top_count)
    columns = jnp.arange(ep_count * capacity, dtype=jnp.int32)
    matches = target[:, :, None] == columns[None, None, :]
    placing = jnp.any(matches, axis=1).astype(jnp.bfloat16)
    weighting = jnp.sum(jnp.where(matches, route_weight[:, :, None], 0.0), axis=1)
    outgoing = lax.dot_general(
        placing, normed, (((0,), (0,)), ((), ())), preferred_element_type=jnp.float32
    ).astype(jnp.bfloat16)
    outgoing = outgoing.reshape(ep_count, capacity, model_width)
    gate_up_weight = unpack_rows(gate_up_codes[0], gate_up_scales[0])
    down_weight = unpack_weights(down_codes[0], down_scales[0])
    arrived = lax.all_to_all(outgoing, "ep", split_axis=0, concat_axis=0, tiled=True)
    source_count, item_count, _ = arrived.shape
    flat_rows = arrived.reshape(source_count * item_count, model_width)
    projected = jnp.dot(
        flat_rows, gate_up_weight, preferred_element_type=jnp.float32
    ) + gate_up_bias[0].astype(jnp.float32)
    gate_part = jnp.minimum(projected[:, 0::2], 7.0)
    upward = jnp.clip(projected[:, 1::2], -7.0, 7.0)
    activated = (gate_part * jax.nn.sigmoid(1.702 * gate_part) * (upward + 1.0)).astype(
        jnp.bfloat16
    )
    partial_value = jnp.dot(activated, down_weight, preferred_element_type=jnp.float32)
    partial_value = partial_value.astype(jnp.bfloat16).astype(jnp.float32)
    partial_value = partial_value.reshape(source_count, item_count, model_width)
    summed = lax.psum_scatter(
        partial_value.astype(jnp.bfloat16), "tp", scatter_dimension=2, tiled=True
    ).astype(jnp.float32)
    answered = (summed + down_bias[0].astype(jnp.float32)).astype(jnp.bfloat16)
    came_back = lax.all_to_all(answered, "ep", split_axis=0, concat_axis=0, tiled=True)
    quarter = model_width // tp_count
    own_cols = lax.dynamic_slice_in_dim(hidden, tp_rank * quarter, quarter, 1).astype(jnp.float32)
    gathered = came_back.reshape(ep_count * capacity, quarter).astype(jnp.float32)
    layer_out = own_cols + jnp.dot(weighting, gathered, precision=lax.Precision.HIGHEST)
    return layer_out.astype(jnp.bfloat16)


def solution(mesh):
    placed = (
        P(("groups", "ep"), None),
        P(("groups", "ep"), None),
        P(("groups", "ep"), None),
        P(),
        P("ep", None, "tp"),
        P("ep", None, "tp"),
        P("ep", "tp"),
        P("ep", "tp", None),
        P("ep", "tp", None),
        P("ep", "tp"),
    )
    return jax.shard_map(
        shards, mesh=mesh, in_specs=placed, out_specs=P(("groups", "ep"), "tp"), check_vma=False
    )
```

profile of v0, /device:TPU:0, one launch (start us, length us, event | category | flops | bytes accessed | tf_op | source)
XLA Modules:
  0.0 424.5 jit_solution(15950444374108988437)
XLA Ops:
  6.5 0.8 copy.46
  7.5 0.6 reduce-window.6
  8.1 0.2 slice_reduce_fusion
  8.7 0.7 multiply_add_fusion
  9.4 0.1 fusion.39
  9.5 0.7 convert_element_type.112
  10.2 1.2 fusion.36
  11.4 2.0 convolution_convert_fusion
  13.4 3.1 copy.49
  16.5 6.4 %all-to-all-start = ((bf16[8,64,2880]{2,1,0:T(8,128)(2,1)}), bf16[8,64,2880]{2,1,0:T(8,128)(2,1)S(1)}, u32[]{:S(2)}, u32[]{:S(2)}) async-start(bf16[8,64,2880]{2,1,0:T(8,128)(2,1)} %bitcast.93), calls=%async_computation | async-start | bytes 6029312 | tf_op jit(solution)/shard_map/all_to_all | solution.py:82
  22.9 0.2 reduce-scatter.4.cloned.1.call-start
  23.2 0.1 shift_right_arithmetic.84
  23.4 6.3 %mul.129 = f32[40,32,2880]{2,1,0:T(8,128)} broadcast(f32[40,2880]{1,0:T(8,128)S(1)} %bitcast_convert_fusion.1), dimensions={0,2} | broadcast | bytes 15206400 | tf_op jit(solution)/shard_map/mul | solution.py:22
  29.7 15.2 %copy.50 = f32[1280,2880]{0,1:T(8,128)} copy(f32[1280,2880]{1,0:T(8,128)} %bitcast.90) | data formatting | bytes 29491200 | tf_op jit(solution)/shard_map/mul | solution.py:22
  45.1 6.5 %shift_right_arithmetic.73 = s32[360,8,2560]{2,1,0:T(8,128)S(1)} broadcast(s32[360,2560]{1,0:T(8,128)} %bitcast.97), dimensions={0,2} | broadcast | bytes 33177600 | tf_op jit(solution)/shard_map/shift_right_arithmetic | solution.py:30
  51.6 19.6 %fusion.1 = bf16[90,32,2560]{2,1,0:T(8,128)(2,1)} fusion(f32[90,2560]{1,0:T(8,128)S(1)} %bitcast_convert_fusion, s32[32]{0:T(128)S(1)} %shift_right_arithmetic.76, s32[90,32,2560]{2,1,0:T(8,128)S(1)} %bitcast.89), kind=kLoop, calls=%fused_computation.4 | loop fusion | flops 132710400 | bytes 45158528 | tf_op jit(solution)/shard_map/convert_element_type | solution.py:36
  71.2 20.4 %all-to-all-done = bf16[8,64,2880]{2,1,0:T(8,128)(2,1)S(1)} async-done(((bf16[8,64,2880]{2,1,0:T(8,128)(2,1)}), bf16[8,64,2880]{2,1,0:T(8,128)(2,1)S(1)}, u32[]{:S(2)}, u32[]{:S(2)}) %all-to-all-start) | async-done | bytes 2949152 | tf_op jit(solution)/shard_map/all_to_all | solution.py:82
  91.6 13.1 %convolution_add_fusion = f32[512,2560]{1,0:T(8,128)} fusion(bf16[512,2880]{1,0:T(8,128)(2,1)S(1)} %bitcast.98, bf16[2880,2560]{1,0:T(8,128)(2,1)} %bitcast.92, f32[2560]{0:T(1024)S(1)} %convert_reduce_fusion), kind=kOutput, calls=%fused_computation.33 | convolution fusion | flops 7551057920 | bytes 22947840 | tf_op jit(solution)/shard_map/dot_general | solution.py:85
  104.7 91.5 %slice.14 = f32[512,1280]{1,0:T(8,128)S(1)} slice(f32[512,2560]{1,0:T(8,128)} %convolution_add_fusion), slice={[0:512:1], [0:2560:2]} | slice | bytes 5242880 | tf_op jit(solution)/shard_map/slice | solution.py:88
  196.2 91.9 %slice.15 = f32[512,1280]{1,0:T(8,128)} slice(f32[512,2560]{1,0:T(8,128)} %convolution_add_fusion), slice={[0:512:1], [1:2560:2]} | slice | bytes 5242880 | tf_op jit(solution)/shard_map/slice | solution.py:89
  288.0 16.8 %fusion.28 = bf16[512,2880]{0,1:T(8,128)(2,1)} fusion(f32[1280,2880]{0,1:T(8,128)} %copy.50, s32[2880]{0:T(1024)S(1)} %shift_right_arithmetic.84, s32[1280,360]{0,1:T(8,128)} %bitcast.99, f32[512,1280]{1,0:T(8,128)} %slice.15, f32[512,1280]{1,0:T(8,128)S(1)} %slice.14), kind=kOutput, calls=%fused_computation.34 | convolution fusion | flops 3849256960 | bytes 24792320 | tf_op jit(solution)/shard_map/dot_general | solution.py:93
  304.8 3.3 copy.51
  308.2 6.0 %copy.52 = bf16[8,64,2880]{1,0,2:T(8,128)(2,1)} copy(bf16[8,64,2880]{2,1,0:T(8,128)(2,1)S(1)} %bitcast.94) | data formatting | bytes 5898240
  314.1 8.9 %reshape.147 = bf16[2880,512]{1,0:T(8,128)(2,1)} reshape(bf16[2880,8,64]{2,1,0:T(8,128)(2,1)} %bitcast.91) | data formatting | bytes 5898240
  323.1 40.3 %reduce-scatter.4.cloned.1.call-done = bf16[1440,512]{1,0:T(8,128)(2,1)} async-done(((bf16[2880,512]{1,0:T(8,128)(2,1)}), bf16[1440,512]{1,0:T(8,128)(2,1)}) %reduce-scatter.4.cloned.1.call-update) | async-done | bytes 1474576
  363.4 3.8 reshape.148
  367.2 3.6 copy.53
  370.8 2.8 add_convert_fusion
  373.6 4.6 %all-to-all-start.1 = ((bf16[8,64,1440]{2,1,0:T(8,128)(2,1)}), bf16[8,64,1440]{2,1,0:T(8,128)(2,1)S(1)}, u32[]{:S(2)}, u32[]{:S(2)}) async-start(bf16[8,64,1440]{2,1,0:T(8,128)(2,1)} %add_convert_fusion), calls=%async_computation.1 | async-start | bytes 3145728 | tf_op jit(solution)/shard_map/all_to_all | solution.py:100
  378.3 0.1 select_reduce_fusion
  378.4 37.7 %all-to-all-done.1 = bf16[8,64,1440]{2,1,0:T(8,128)(2,1)S(1)} async-done(((bf16[8,64,1440]{2,1,0:T(8,128)(2,1)}), bf16[8,64,1440]{2,1,0:T(8,128)(2,1)S(1)}, u32[]{:S(2)}, u32[]{:S(2)}) %all-to-all-start.1) | async-done | bytes 1474592 | tf_op jit(solution)/shard_map/all_to_all | solution.py:100
  416.1 1.6 fusion.31
  (30 shorter events, 0.8 us)
Async XLA Ops:
  13.4 9.9 %copy-start.2 = (bf16[1,40,2880]{2,1,0:T(8,128)(2,1)S(1)}, bf16[1,40,2880]{2,1,0:T(8,128)(2,1)}, u32[]{:S(2)}) copy-start(bf16[1,40,2880]{2,1,0:T(8,128)(2,1)} %param.18) | copy-start | bytes 691204
  16.5 75.0 %all-to-all-start = ((bf16[8,64,2880]{2,1,0:T(8,128)(2,1)}), bf16[8,64,2880]{2,1,0:T(8,128)(2,1)S(1)}, u32[]{:S(2)}, u32[]{:S(2)}) async-start(bf16[8,64,2880]{2,1,0:T(8,128)(2,1)} %bitcast.93), calls=%async_computation | async-start | bytes 6029312 | tf_op jit(solution)/shard_map/all_to_all | solution.py:82
  22.9 340.5 %reduce-scatter.4.cloned.1.call-start = ((), (), s32[]{:S(2)}) async-start(), calls=%async_computation.3 | async-start | bytes 4423680
  29.7 15.3 %copy-start.3 = (bf16[1,2560]{1,0:T(2,128)(2,1)S(1)}, bf16[1,2560]{1,0:T(2,128)(2,1)}, u32[]{:S(2)}) copy-start(bf16[1,2560]{1,0:T(2,128)(2,1)} %param.16) | copy-start | bytes 15364
  29.7 15.3 %copy-start.1 = (bf16[1,90,2560]{2,1,0:T(8,128)(2,1)S(1)}, bf16[1,90,2560]{2,1,0:T(8,128)(2,1)}, u32[]{:S(2)}) copy-start(bf16[1,90,2560]{2,1,0:T(8,128)(2,1)} %param.15) | copy-start | bytes 1382404
  314.1 8.9 %copy-start.4 = (bf16[1,1440]{1,0:T(2,128)(2,1)S(1)}, bf16[1,1440]{1,0:T(2,128)(2,1)}, u32[]{:S(2)}) copy-start(bf16[1,1440]{1,0:T(2,128)(2,1)} %param.19) | copy-start | bytes 8644
  323.1 55.2 %copy-start.5 = (f32[64,4]{0,1:T(4,128)S(1)}, f32[64,4]{0,1:T(4,128)}, u32[]{:S(2)}) copy-start(f32[64,4]{0,1:T(4,128)} %param.12) | copy-start | bytes 3076
  323.1 92.9 %copy-start = (bf16[64,2880]{1,0:T(8,128)(2,1)S(1)}, bf16[64,2880]{1,0:T(8,128)(2,1)}, u32[]{:S(2)}) copy-start(bf16[64,2880]{1,0:T(8,128)(2,1)} %param.10) | copy-start | bytes 1105924
  373.6 42.4 %all-to-all-start.1 = ((bf16[8,64,1440]{2,1,0:T(8,128)(2,1)}), bf16[8,64,1440]{2,1,0:T(8,128)(2,1)S(1)}, u32[]{:S(2)}, u32[]{:S(2)}) async-start(bf16[8,64,1440]{2,1,0:T(8,128)(2,1)} %add_convert_fusion), calls=%async_computation.1 | async-start | bytes 3145728 | tf_op jit(solution)/shard_map/all_to_all | solution.py:100
Sparse Core Ops, SparseCore 0:
  323.2 40.1 reduce-scatter.3
where the time goes:
time: 426 us; the launch traced here: 424 us
  local copies, waits for them, and re-layouts  242 us (57%)
  waiting for transfers between devices  98.3 us (23%)
  matrix products  33.6 us (8%)
  other arithmetic  26.2 us (6%)
  between operations  13.6 us (3%)
  starting transfers between devices  11.2 us (3%)
    slice x1, local copies, waits for them, and re-layouts, shards(): upward = jnp.clip(projected[:, 1::2], -7.0, 7.0)  91.9 us
    slice x1, local copies, waits for them, and re-layouts, shards(): gate_part = jnp.minimum(projected[:, 0::2], 7.0)  91.5 us
    unnamed x2, waiting for transfers between devices  40.3 us
    all_to_all x1, waiting for transfers between devices, shards(): lax.all_to_all(answered, 'ep', split_axis=0, concat_axis=0, tiled=True)  37.7 us
    unnamed x17, local copies, waits for them, and re-layouts  23 us
    mul x2, local copies, waits for them, and re-layouts, unpack_weights(): signed_val.reshape(row_count // 32, 32, -1)  21.6 us
    all_to_all x1, waiting for transfers between devices, shards(): lax.all_to_all(outgoing, 'ep', split_axis=0, concat_axis=0, tiled=True)  20.4 us
    convert_element_type x1, other arithmetic, unpack_rows(): return signed_val.reshape(row_count, -1).astype(jnp.bfloat16)  19.6 us
  transfers between devices with their start and end apart: 3, of which 3 were waited for; matrix products, arithmetic and copies ran while one was open for 11% of the time, Pallas kernels for 0%

commit v1 on v0

--- a/solution.py
+++ b/solution.py
@@ -1,7 +1,14 @@
+import functools
+
 import jax
 import jax.numpy as jnp
 from jax import lax
+from jax.experimental import pallas as pl
+from jax.experimental.pallas import tpu as pltpu
 from jax.sharding import PartitionSpec as P
+
+MAGNITUDES = 0xC8643210 - (1 << 32)
+SPARE = 64
 
 
 def decode_nibble(nibble):
@@ -105,7 +112,403 @@
     return layer_out.astype(jnp.bfloat16)
 
 
+def xor_peer(z, d):
+    if d & 1:
+        z = z + 1 - 2 * (z % 2)
+    if d & 2:
+        z = z + 2 - 4 * ((z // 2) % 2)
+    return z
+
+
+def layer_kernel(
+    sizes,
+    payload,
+    own_cols,
+    gate_codes,
+    gate_scales,
+    gate_bias,
+    down_codes,
+    down_scales,
+    down_bias,
+    out,
+    rows_in,
+    gate_weight,
+    down_weight,
+    padded_codes,
+    activated,
+    pair_out,
+    pair_in,
+    side_out,
+    side_in,
+    kept,
+    far_out,
+    far_in,
+    own_send,
+    own_recv,
+    disp_send,
+    disp_recv,
+    cross_send,
+    cross_recv,
+    fwd_send,
+    fwd_recv,
+    pair_send,
+    pair_recv,
+    side_send,
+    side_recv,
+    far_send,
+    far_recv,
+):
+    tok, width, n_z = sizes
+    half_rows = tok // 2
+    half_cols = width // 2
+    ep = lax.axis_index("ep")
+    x = lax.axis_index("tp")
+    z = ep // 2
+    core = ep % 2
+    partner = {"ep": 2 * z + 1 - core}
+    across = {"tp": 1 - x}
+
+    def far(d):
+        return {"ep": 2 * xor_peer(z, d) + core}
+
+    def copy(src, dst, send, recv, device):
+        return pltpu.make_async_remote_copy(
+            src_ref=src,
+            dst_ref=dst,
+            send_sem=send,
+            recv_sem=recv,
+            device_id=device,
+            device_id_type=pl.DeviceIdType.MESH,
+        )
+
+    barrier = pltpu.get_barrier_semaphore()
+    for device in [partner, across] + [far(d) for d in range(1, n_z)]:
+        pl.semaphore_signal(
+            barrier, inc=1, device_id=device, device_id_type=pl.DeviceIdType.MESH
+        )
+    pl.semaphore_wait(barrier, n_z + 1)
+
+    def block_rows(owner, half=None):
+        if half is None:
+            return rows_in.at[pl.ds(pl.multiple_of(owner * tok, tok), tok)]
+        start = owner * tok + half * half_rows
+        return rows_in.at[pl.ds(pl.multiple_of(start, half_rows), half_rows)]
+
+    own_half = payload.at[pl.ds(pl.multiple_of(x * half_rows, half_rows), half_rows)]
+    disp = [
+        copy(own_half, block_rows(ep, x), disp_send.at[d], disp_recv.at[d], far(d))
+        for d in range(1, n_z)
+    ]
+    own = copy(payload, block_rows(ep), own_send, own_recv, partner)
+    for step in disp:
+        step.start()
+    own.start()
+    rows_in[pl.ds(pl.multiple_of(ep * tok, tok), tok), :] = payload[...]
+
+    def arriving(d, half):
+        return block_rows(2 * xor_peer(z, d) + core, half)
+
+    crossing = [
+        copy(arriving(d, x), arriving(d, x), cross_send.at[d], cross_recv.at[d], across)
+        for d in range(1, n_z)
+    ]
+    passing = [
+        [
+            copy(arriving(d, h), arriving(d, h), fwd_send.at[d, i], fwd_recv.at[d, i], partner)
+            for i, h in enumerate((x, 1 - x))
+        ]
+        for d in range(1, n_z)
+    ]
+
+    def pass_on(d):
+        disp[d - 1].wait_recv()
+        crossing[d - 1].start()
+        passing[d - 1][0].start()
+
+    def pass_crossed(d):
+        crossing[d - 1].wait_recv()
+        passing[d - 1][1].start()
+
+    place = lax.broadcasted_iota(jnp.int32, (8, 1), 0) * 4
+    gate_cols = gate_codes.shape[1]
+    col_step = 512 if gate_cols % 512 == 0 else 256
+
+    def gate_rows(s, carry):
+        base = pl.multiple_of(s * 8, 8)
+        for col in range(0, gate_cols, col_step):
+            words = gate_codes[pl.ds(base, 8), col : col + col_step]
+            shifted = words
+            for group in range(2):
+                scale = jnp.broadcast_to(
+                    gate_scales[pl.ds(2 * s + group, 1), col : col + col_step], (8, col_step)
+                )
+                pieces = []
+                for w in range(4):
+                    row = group * 4 + w
+                    one = jnp.broadcast_to(shifted[row : row + 1, :], (8, col_step))
+                    place_wide = jnp.broadcast_to(place, (8, col_step))
+                    quad = jnp.left_shift(lax.shift_right_logical(one, place_wide), 2) & 28
+                    doubled = lax.shift_right_logical(jnp.full_like(one, MAGNITUDES), quad) & 15
+                    negative = jnp.left_shift(one, 28 - place_wide) < 0
+                    pieces.append(
+                        doubled.astype(jnp.float32) * jnp.where(negative, -scale, scale)
+                    )
+                start = pl.multiple_of(s * 64 + group * 32, 32)
+                gate_weight[pl.ds(start, 32), col : col + col_step] = jnp.concatenate(
+                    pieces, axis=0
+                ).astype(jnp.bfloat16)
+        return carry
+
+    gate_steps = gate_codes.shape[0] // 8
+    gate_weight[pl.ds(width, SPARE), :] = jnp.zeros((SPARE, gate_cols), jnp.bfloat16)
+    cut = gate_steps // 2
+    lax.fori_loop(0, cut, gate_rows, 0)
+    pass_on(1)
+    lax.fori_loop(cut, gate_steps, gate_rows, 0)
+    pass_on(2)
+    pass_crossed(1)
+
+    code_words = down_codes.shape[1]
+    whole_lanes = code_words // 128 * 128
+    lane_total = padded_codes.shape[1]
+    padded_codes[:, lane_total - 128 :] = jnp.zeros((padded_codes.shape[0], 128), jnp.int32)
+    padded_codes[:, 0:whole_lanes] = down_codes[:, 0:whole_lanes]
+    padded_codes[:, whole_lanes:code_words] = down_codes[:, whole_lanes:code_words]
+    lanes = lax.broadcasted_iota(jnp.int32, (32, 128), 1)
+    lane_word = lanes // 8
+    lane_place = (lanes % 8) * 4
+    lane_sign = 28 - lane_place
+
+    down_steps = down_codes.shape[0] // 32
+
+    def down_rows(h, s, carry):
+        base = pl.multiple_of(s * 32, 32)
+        sources = [
+            padded_codes[pl.ds(base, 32), v * 128 : (v + 1) * 128] for v in range(lane_total // 128)
+        ]
+        scale_row = down_scales[pl.ds(h * down_steps + s, 1), :]
+        for b in range(-(-half_cols // 128)):
+            first = h * (half_cols // 8) + 16 * b
+            low, high = first // 128, (first + 15) // 128
+            index = (lane_word + first % 128) % 128
+            words = jnp.take_along_axis(sources[low], index, axis=1, mode="promise_in_bounds")
+            if high != low:
+                other = jnp.take_along_axis(sources[high], index, axis=1, mode="promise_in_bounds")
+                words = jnp.where(lane_word + first % 128 < 128, words, other)
+            size = min(128, half_cols - 128 * b)
+            scale = jnp.broadcast_to(scale_row[:, 128 * b : 128 * (b + 1)], (32, 128))
+            quad = jnp.left_shift(lax.shift_right_logical(words, lane_place), 2) & 28
+            doubled = lax.shift_right_logical(jnp.full_like(words, MAGNITUDES), quad) & 15
+            negative = jnp.left_shift(words, lane_sign) < 0
+            value = (doubled.astype(jnp.float32) * jnp.where(negative, -scale, scale)).astype(
+                jnp.bfloat16
+            )
+            down_weight[h, pl.ds(base, 32), 128 * b : 128 * b + size] = value[:, :size]
+        return carry
+
+    lax.fori_loop(0, down_steps, functools.partial(down_rows, 0), 0)
+    pass_on(3)
+    pass_crossed(2)
+    lax.fori_loop(0, down_steps, functools.partial(down_rows, 1), 0)
+    pass_crossed(3)
+    own.wait_recv()
+    for d in range(1, n_z):
+        for step in passing[d - 1]:
+            step.wait_recv()
+
+    picks = (
+        lax.broadcasted_iota(jnp.int32, (256, 128), 0)
+        == 2 * lax.broadcasted_iota(jnp.int32, (256, 128), 1)
+    ).astype(jnp.float32).astype(jnp.bfloat16)
+
+    def gate_tile(t, carry):
+        cols = pl.ds(pl.multiple_of(t * 256, 256), 256)
+        projected = jnp.dot(
+            rows_in[...], gate_weight[:, cols], preferred_element_type=jnp.float32
+        ) + gate_bias[:, cols]
+        gate_part = jnp.minimum(projected, 7.0)
+        upward = pltpu.roll(jnp.clip(projected, -7.0, 7.0), 255, 1)
+        value = gate_part * jax.nn.sigmoid(1.702 * gate_part) * (upward + 1.0)
+        activated[:, pl.ds(pl.multiple_of(t * 128, 128), 128)] = jnp.dot(
+            value.astype(jnp.bfloat16), picks, preferred_element_type=jnp.float32
+        ).astype(jnp.bfloat16)
+        return carry
+
+    lax.fori_loop(0, gate_cols // 256, gate_tile, 0)
+
+    tail = lax.broadcasted_iota(jnp.int32, (2 * tok, SPARE), 1)
+    pairing = [
+        copy(pair_out.at[d], pair_in.at[d], pair_send.at[d], pair_recv.at[d], partner)
+        for d in range(n_z)
+    ]
+    siding = [
+        copy(side_out.at[d], side_in.at[d], side_send.at[d], side_recv.at[d], across)
+        for d in range(n_z)
+    ]
+    faring = [
+        None if d == 0 else copy(far_out.at[d], far_in.at[d], far_send.at[d], far_recv.at[d], far(d))
+        for d in range(n_z)
+    ]
+
+    def multiply(d):
+        start = pl.multiple_of(xor_peer(z, d) * 2 * tok, 2 * tok)
+        rows = activated[pl.ds(start, 2 * tok), :]
+        spare = rows_in[pl.ds(start, 2 * tok), width:].astype(jnp.float32)
+        hit = (tail == ep) | (tail == ep + 2 * n_z) | (tail == ep + 4 * n_z)
+        weight = jnp.sum(jnp.where(hit, spare, 0.0), axis=1, keepdims=True)
+        for h in range(2):
+            added = down_bias[...] * jnp.where(x == h, 1.0, 0.0)
+            value = jnp.dot(rows, down_weight[h], preferred_element_type=jnp.float32) + added
+            value = value * weight
+            first, second = value[:tok], value[tok:]
+            pair_out[d, h] = jnp.where(core == 0, second, first).astype(jnp.bfloat16)
+            kept[d, h] = jnp.where(core == 0, first, second).astype(jnp.bfloat16)
+        pairing[d].start()
+
+    def fold_pair(d):
+        pairing[d].wait_recv()
+        sums = [
+            kept[d, h].astype(jnp.float32) + pair_in[d, h].astype(jnp.float32) for h in range(2)
+        ]
+        side_out[d] = jnp.where(x == 0, sums[1], sums[0]).astype(jnp.bfloat16)
+        kept[d, 0] = jnp.where(x == 0, sums[0], sums[1]).astype(jnp.bfloat16)
+        siding[d].start()
+
+    def fold_side(d):
+        siding[d].wait_recv()
+        total = kept[d, 0].astype(jnp.float32) + side_in[d].astype(jnp.float32)
+        if d == 0:
+            return total
+        far_out[d] = total.astype(jnp.bfloat16)
+        faring[d].start()
+        return None
+
+    multiply(3)
+    multiply(2)
+    fold_pair(3)
+    multiply(1)
+    fold_pair(2)
+    multiply(0)
+    fold_pair(1)
+    fold_side(3)
+    fold_pair(0)
+    fold_side(2)
+    fold_side(1)
+    total = fold_side(0) + own_cols[...].astype(jnp.float32)
+    for d in (3, 2, 1):
+        faring[d].wait_recv()
+        total = total + far_in[d].astype(jnp.float32)
+    out[...] = total.astype(jnp.bfloat16)
+
+    own.wait_send()
+    for d in range(1, n_z):
+        disp[d - 1].wait_send()
+        crossing[d - 1].wait_send()
+        for step in passing[d - 1]:
+            step.wait_send()
+        faring[d].wait_send()
+    for d in range(n_z):
+        pairing[d].wait_send()
+        siding[d].wait_send()
+
+
+def dense_shards(
+    hidden,
+    route_experts,
+    route_weight,
+    norm_gain,
+    gate_up_codes,
+    gate_up_scales,
+    gate_up_bias,
+    down_codes,
+    down_scales,
+    down_bias,
+):
+    ep_count = lax.axis_size("ep")
+    tp_rank = lax.axis_index("tp")
+    tok, width = hidden.shape
+    n_z = ep_count // 2
+    half = width // 2
+    normed = rms_normed(hidden, norm_gain)
+    experts = jnp.arange(ep_count, dtype=jnp.int32)
+    per_expert = jnp.sum(
+        jnp.where(
+            route_experts[:, :, None] == experts[None, None, :], route_weight[:, :, None], 0.0
+        ),
+        axis=1,
+    )
+    high = lax.reduce_precision(per_expert, 8, 7)
+    middle = lax.reduce_precision(per_expert - high, 8, 7)
+    low = per_expert - high - middle
+    spare = jnp.concatenate(
+        [high, middle, low, jnp.zeros((tok, SPARE - 3 * ep_count), jnp.float32)], axis=1
+    ).astype(jnp.bfloat16)
+    payload = jnp.concatenate([normed, spare], axis=1)
+    own_cols = lax.dynamic_slice_in_dim(hidden, tp_rank * half, half, 1)
+    gate_scales = gate_up_scales[0].astype(jnp.float32) * 0.5
+    units = down_codes.shape[1]
+    lanes = -(-half // 128) * 128
+    halves = (down_scales[0].astype(jnp.float32) * 0.5).reshape(-1, 2, half).transpose(1, 0, 2)
+    halves = jnp.pad(halves, ((0, 0), (0, 0), (0, lanes - half))).reshape(-1, lanes)
+    code_lanes = -(-down_codes.shape[2] // 128) * 128
+    bf16 = jnp.bfloat16
+    dma = pltpu.SemaphoreType.DMA
+    vmem = pltpu.VMEM
+    return pl.pallas_call(
+        functools.partial(layer_kernel, (tok, width, n_z)),
+        out_shape=jax.ShapeDtypeStruct((tok, half), bf16),
+        in_specs=[pl.BlockSpec(memory_space=vmem)] * 8,
+        out_specs=pl.BlockSpec(memory_space=vmem),
+        scratch_shapes=[
+            vmem((ep_count * tok, width + SPARE), bf16),
+            vmem((width + SPARE, gate_up_codes.shape[2]), bf16),
+            vmem((2, units, half), bf16),
+            vmem((units, code_lanes), jnp.int32),
+            vmem((ep_count * tok, units), bf16),
+            vmem((n_z, 2, tok, half), bf16),
+            vmem((n_z, 2, tok, half), bf16),
+            vmem((n_z, tok, half), bf16),
+            vmem((n_z, tok, half), bf16),
+            vmem((n_z, 2, tok, half), bf16),
+            vmem((n_z, tok, half), bf16),
+            vmem((n_z, tok, half), bf16),
+            dma,
+            dma,
+            dma((n_z,)),
+            dma((n_z,)),
+            dma((n_z,)),
+            dma((n_z,)),
+            dma((n_z, 2)),
+            dma((n_z, 2)),
+            dma((n_z,)),
+            dma((n_z,)),
+            dma((n_z,)),
+            dma((n_z,)),
+            dma((n_z,)),
+            dma((n_z,)),
+        ],
+        compiler_params=pltpu.CompilerParams(
+            collective_id=0, has_side_effects=True, vmem_limit_bytes=63 * 1024 * 1024
+        ),
+    )(
+        payload,
+        own_cols,
+        gate_up_codes[0],
+        gate_scales,
+        gate_up_bias.astype(jnp.float32),
+        down_codes[0],
+        halves,
+        down_bias.astype(jnp.float32),
+    )
+
+
 def solution(mesh):
+    def layer(*arrays):
+        tok, top = arrays[1].shape
+        ep_count, tp_count = lax.axis_size("ep"), lax.axis_size("tp")
+        dense = 2 * top >= ep_count and tp_count == 2 and ep_count == 8
+        return (dense_shards if dense else shards)(*arrays)
+
     placed = (
         P(("groups", "ep"), None),
         P(("groups", "ep"), None),
@@ -119,5 +522,5 @@
         P("ep", "tp"),
     )
     return jax.shard_map(
-        shards, mesh=mesh, in_specs=placed, out_specs=P(("groups", "ep"), "tp"), check_vma=False
-    )
+        layer, mesh=mesh, in_specs=placed, out_specs=P(("groups", "ep"), "tp"), check_vma=False
+    )

time: 426 us -> 93.6 us (0.22)
  local copies, waits for them, and re-layouts: 242 us -> 7.76 us
  waiting for transfers between devices: 98.3 us -> 0 us
  Pallas kernels: 0 us -> 77.9 us
  matrix products: 33.6 us -> 0 us
  other arithmetic: 26.2 us -> 7.47 us
  between operations: 13.6 us -> 0.07 us
  starting transfers between devices: 11.2 us -> 0 us
    slice x3 -> x0, local copies, waits for them, and re-layouts: 184 us -> none  [the longest x1 91.9 us: shards(): upward = jnp.clip(projected[:, 1::2], -7.0, 7.0)]
    pallas_call x0 -> x1, Pallas kernels: none -> 77.9 us  [dense_shards(): pl.pallas_call(functools.partial(layer_kernel, (tok, width, n_z)), out_sh...]
    all_to_all x2 -> x0, waiting for transfers between devices: 58 us -> none  [the longest x1 37.7 us: shards(): lax.all_to_all(answered, 'ep', split_axis=0, concat_axis=0, tiled=True)]
    unnamed x2 -> x0, waiting for transfers between devices: 40.3 us -> none
    dot_general x4 -> x0, matrix products: 33.6 us -> none  [the longest x1 16.8 us: shards(): jnp.dot(activated, down_weight, preferred_element_type=jnp.float32)]
    mul x2, local copies, waits for them, and re-layouts: 21.6 us -> 0.62 us  [dense_shards(): down_scales[0].astype(jnp.float32) * 0.5]
    unnamed x17 -> x8, local copies, waits for them, and re-layouts: 23 us -> 3.43 us
    convert_element_type x6 -> x3, other arithmetic: 22.6 us -> 3.74 us  [the longest x1 1.3 us: dense_shards(): gate_up_bias.astype(jnp.float32)]
  transfers between devices with their start and end apart: 3 -> 0, of which waited for: 3 -> 0; matrix products, arithmetic and copies ran while one was open for 11% -> 0% of each run, Pallas kernels for 0% -> 0%
where the time goes in v1:
time: 93.6 us; the launch traced here: 93.2 us
  Pallas kernels  77.9 us (83%)
  local copies, waits for them, and re-layouts  7.76 us (8%)
  other arithmetic  7.47 us (8%)
    pallas_call x1, Pallas kernels, dense_shards(): pl.pallas_call(functools.partial(layer_kernel, (tok, width, n_z)), out_sh...  77.9 us
    unnamed x8, local copies, waits for them, and re-layouts  3.43 us

profile of v1, /device:TPU:0, one launch (start us, length us, event | category | flops | bytes accessed | tf_op | source)
XLA Modules:
  0.0 93.2 jit_solution(4278936091927071293)
XLA Ops:
  0.0 0.0 copy-start.2
  0.0 1.2 %fusion = f32[64]{0:T(128)S(1)} fusion(bf16[64,2880]{1,0:T(8,128)(2,1)} %param.10), kind=kLoop, calls=%fused_computation.3 | loop fusion | flops 552896 | bytes 368896 | tf_op jit(solution)/shard_map/reduce_sum | solution.py:48
  1.2 0.7 select_reduce_fusion
  1.9 1.3 %convert_element_type.33.down_bias = f32[1,1440]{1,0:T(1,128)} convert(bf16[1,1440]{1,0:T(2,128)(2,1)} %param.19) | non-fusion elementwise | flops 1440 | bytes 8640 | tf_op jit(solution)/shard_map/convert_element_type | solution.py:501
  3.2 1.3 %convert_element_type.31.gate_bias = f32[1,2560]{1,0:T(1,128)} convert(bf16[1,2560]{1,0:T(2,128)(2,1)} %param.16) | non-fusion elementwise | flops 2560 | bytes 15360 | tf_op jit(solution)/shard_map/convert_element_type | solution.py:498
  4.5 0.7 convert_element_type.28
  5.2 0.1 copy.21
  5.3 0.1 copy.20
  5.4 0.1 copy.19
  5.5 1.7 %constant_dynamic-slice_fusion.own_cols = bf16[64,1440]{1,0:T(8,128)(2,1)} fusion(bf16[64,2880]{1,0:T(8,128)(2,1)} %param.10, s32[]{:T(128)S(6)} %select_n.8), kind=kLoop, calls=%fused_computation.14 | loop fusion | bytes 368644 | tf_op jit(solution)/shard_map/dynamic_slice | solution.py:447
  7.3 1.1 %fusion.2 = bf16[64,2880]{1,0:T(8,128)(2,1)S(1)} fusion(bf16[64,2880]{1,0:T(8,128)(2,1)} %param.10, f32[2880]{0:T(1024)S(1)} %convert_element_type.28, f32[64]{0:T(128)S(1)} %add_rsqrt_fusion), kind=kLoop, calls=%fused_computation.5 | loop fusion | flops 737280 | bytes 749056 | tf_op jit(solution)/shard_map/convert_element_type | solution.py:50
  8.4 0.9 concatenate.6.payload
  9.3 0.0 copy-done.2
  9.3 0.0 copy-start.1
  9.3 0.0 copy-start
  9.3 0.5 mul.51
  9.9 0.1 copy.25
  10.0 0.8 pad.4
  10.8 0.0 copy-done.1
  10.8 1.1 %multiply_bitcast_fusion.gate_scales = f32[90,2560]{1,0:T(8,128)} fusion(bf16[1,90,2560]{2,1,0:T(8,128)(2,1)S(1)} %copy-done.1), kind=kLoop, calls=%fused_computation | loop fusion | flops 460800 | bytes 1382400 | tf_op jit(solution)/shard_map/mul | solution.py:448
  11.9 0.0 copy-done
  11.9 1.8 %copy.22 = s32[1,1280,360]{2,1,0:T(8,128)} copy(s32[1,1280,360]{1,2,0:T(8,128)S(1)} %copy-done) | data formatting | bytes 3686400 | tf_op args[7]
  13.7 77.9 %shard_map.100 = bf16[64,1440]{1,0:T(8,128)(2,1)} custom-call(bf16[64,2944]{1,0:T(8,128)(2,1)} %concatenate.6.payload, bf16[64,1440]{1,0:T(8,128)(2,1)} %constant_dynamic-slice_fusion.own_cols, s32[360,2560]{1,0:T(8,128)} %bitcast.9, f32[90,2560]{1,0:T(8,128)} %multiply_bitcast_fusion.gate_scales, f32[1,2560]{1,0:T(1,128)} %convert_element_type.31.gate_bias, ...), custom_call_target="tpu_custom_call" | custom-call | tf_op jit(solution)/shard_map/pallas_call | solution.py:457
  91.6 1.6 %copy.27 = bf16[64,1440]{1,0:T(8,128)(2,1)} copy(bf16[64,1440]{1,0:T(8,128)(2,1)} %shard_map.100) | data formatting | bytes 368640
  (5 shorter events, 0.1 us)
Async XLA Ops:
  0.0 9.3 %copy-start.2 = (bf16[1,40,2880]{2,1,0:T(8,128)(2,1)S(1)}, bf16[1,40,2880]{2,1,0:T(8,128)(2,1)}, u32[]{:S(2)}) copy-start(bf16[1,40,2880]{2,1,0:T(8,128)(2,1)} %param.18) | copy-start | bytes 691204
  9.3 1.5 %copy-start.1 = (bf16[1,90,2560]{2,1,0:T(8,128)(2,1)S(1)}, bf16[1,90,2560]{2,1,0:T(8,128)(2,1)}, u32[]{:S(2)}) copy-start(bf16[1,90,2560]{2,1,0:T(8,128)(2,1)} %param.15) | copy-start | bytes 1382404
  9.3 2.5 %copy-start = (s32[1,1280,360]{1,2,0:T(8,128)S(1)}, s32[1,1280,360]{1,2,0:T(8,128)}, u32[]{:S(2)}) copy-start(s32[1,1280,360]{1,2,0:T(8,128)} %param.17) | copy-start | bytes 5529604

commit v2 on v1

--- a/solution.py
+++ b/solution.py
@@ -122,15 +122,20 @@
 
 def layer_kernel(
     sizes,
-    payload,
-    own_cols,
+    hidden,
+    routes,
+    route_weights,
+    gain,
     gate_codes,
-    gate_scales,
+    gate_scales_in,
     gate_bias,
     down_codes,
-    down_scales,
+    down_scales_in,
     down_bias,
     out,
+    payload,
+    gate_scales,
+    down_scales,
     rows_in,
     gate_weight,
     down_weight,
@@ -181,6 +186,29 @@
             device_id_type=pl.DeviceIdType.MESH,
         )
 
+    widened = hidden[...].astype(jnp.float32)
+    mean_square = jnp.mean(widened * widened, axis=-1, keepdims=True)
+    normed = (widened * lax.rsqrt(mean_square + 1e-05) * gain[...].astype(jnp.float32)).astype(
+        jnp.bfloat16
+    )
+    lane = lax.broadcasted_iota(jnp.int32, (tok, SPARE), 1)
+    weight_at = jnp.zeros((tok, SPARE), jnp.float32)
+    for k in range(routes.shape[1]):
+        chosen = routes[:, k : k + 1] == lane % (2 * n_z)
+        weight_at = weight_at + jnp.where(chosen, route_weights[:, k : k + 1], 0.0)
+    high = weight_at.astype(jnp.bfloat16).astype(jnp.float32)
+    middle = (weight_at - high).astype(jnp.bfloat16).astype(jnp.float32)
+    low = weight_at - high - middle
+    piece = lane // (2 * n_z)
+    spare_lanes = jnp.where(
+        piece == 0, high, jnp.where(piece == 1, middle, jnp.where(piece == 2, low, 0.0))
+    )
+    aligned = width // 128 * 128
+    payload[:, :aligned] = normed[:, :aligned]
+    payload[:, aligned:] = jnp.concatenate(
+        [normed[:, aligned:], spare_lanes.astype(jnp.bfloat16)], axis=1
+    )
+
     barrier = pltpu.get_barrier_semaphore()
     for device in [partner, across] + [far(d) for d in range(1, n_z)]:
         pl.semaphore_signal(
@@ -229,6 +257,13 @@
         crossing[d - 1].wait_recv()
         passing[d - 1][1].start()
 
+    gate_scales[...] = gate_scales_in[...].astype(jnp.float32) * 0.5
+    scale_rows, scale_lanes = down_scales_in.shape[0], down_scales.shape[1]
+    down_scales[:, scale_lanes - 128 :] = jnp.zeros((2 * scale_rows, 128), jnp.float32)
+    for h in range(2):
+        down_scales[h * scale_rows : (h + 1) * scale_rows, :half_cols] = (
+            down_scales_in[:, h * half_cols : (h + 1) * half_cols].astype(jnp.float32) * 0.5
+        )
     place = lax.broadcasted_iota(jnp.int32, (8, 1), 0) * 4
     gate_cols = gate_codes.shape[1]
     col_step = 512 if gate_cols % 512 == 0 else 256
@@ -311,10 +346,6 @@
     pass_crossed(2)
     lax.fori_loop(0, down_steps, functools.partial(down_rows, 1), 0)
     pass_crossed(3)
-    own.wait_recv()
-    for d in range(1, n_z):
-        for step in passing[d - 1]:
-            step.wait_recv()
 
     picks = (
         lax.broadcasted_iota(jnp.int32, (256, 128), 0)
@@ -325,7 +356,7 @@
         cols = pl.ds(pl.multiple_of(t * 256, 256), 256)
         projected = jnp.dot(
             rows_in[...], gate_weight[:, cols], preferred_element_type=jnp.float32
-        ) + gate_bias[:, cols]
+        ) + gate_bias[:, cols].astype(jnp.float32)
         gate_part = jnp.minimum(projected, 7.0)
         upward = pltpu.roll(jnp.clip(projected, -7.0, 7.0), 255, 1)
         value = gate_part * jax.nn.sigmoid(1.702 * gate_part) * (upward + 1.0)
@@ -334,7 +365,6 @@
         ).astype(jnp.bfloat16)
         return carry
 
-    lax.fori_loop(0, gate_cols // 256, gate_tile, 0)
 
     tail = lax.broadcasted_iota(jnp.int32, (2 * tok, SPARE), 1)
     pairing = [
@@ -357,7 +387,7 @@
         hit = (tail == ep) | (tail == ep + 2 * n_z) | (tail == ep + 4 * n_z)
         weight = jnp.sum(jnp.where(hit, spare, 0.0), axis=1, keepdims=True)
         for h in range(2):
-            added = down_bias[...] * jnp.where(x == h, 1.0, 0.0)
+            added = down_bias[...].astype(jnp.float32) * jnp.where(x == h, 1.0, 0.0)
             value = jnp.dot(rows, down_weight[h], preferred_element_type=jnp.float32) + added
             value = value * weight
             first, second = value[:tok], value[tok:]
@@ -383,19 +413,28 @@
         faring[d].start()
         return None
 
+    def gathered(d):
+        for step in passing[d - 1]:
+            step.wait_recv()
+
+    own.wait_recv()
+    for d in range(1, n_z):
+        gathered(d)
+    lax.fori_loop(0, gate_cols // 256, gate_tile, 0)
     multiply(3)
     multiply(2)
     fold_pair(3)
     multiply(1)
     fold_pair(2)
+    fold_side(3)
     multiply(0)
     fold_pair(1)
-    fold_side(3)
+    fold_side(2)
     fold_pair(0)
-    fold_side(2)
     fold_side(1)
-    total = fold_side(0) + own_cols[...].astype(jnp.float32)
-    for d in (3, 2, 1):
+    own_cols = jnp.where(x == 0, hidden[:, :half_cols], hidden[:, half_cols:])
+    total = fold_side(0) + own_cols.astype(jnp.float32)
+    for d in (1, 3, 2):
         faring[d].wait_recv()
         total = total + far_in[d].astype(jnp.float32)
     out[...] = total.astype(jnp.bfloat16)
@@ -425,31 +464,11 @@
     down_bias,
 ):
     ep_count = lax.axis_size("ep")
-    tp_rank = lax.axis_index("tp")
     tok, width = hidden.shape
     n_z = ep_count // 2
     half = width // 2
-    normed = rms_normed(hidden, norm_gain)
-    experts = jnp.arange(ep_count, dtype=jnp.int32)
-    per_expert = jnp.sum(
-        jnp.where(
-            route_experts[:, :, None] == experts[None, None, :], route_weight[:, :, None], 0.0
-        ),
-        axis=1,
-    )
-    high = lax.reduce_precision(per_expert, 8, 7)
-    middle = lax.reduce_precision(per_expert - high, 8, 7)
-    low = per_expert - high - middle
-    spare = jnp.concatenate(
-        [high, middle, low, jnp.zeros((tok, SPARE - 3 * ep_count), jnp.float32)], axis=1
-    ).astype(jnp.bfloat16)
-    payload = jnp.concatenate([normed, spare], axis=1)
-    own_cols = lax.dynamic_slice_in_dim(hidden, tp_rank * half, half, 1)
-    gate_scales = gate_up_scales[0].astype(jnp.float32) * 0.5
     units = down_codes.shape[1]
     lanes = -(-half // 128) * 128
-    halves = (down_scales[0].astype(jnp.float32) * 0.5).reshape(-1, 2, half).transpose(1, 0, 2)
-    halves = jnp.pad(halves, ((0, 0), (0, 0), (0, lanes - half))).reshape(-1, lanes)
     code_lanes = -(-down_codes.shape[2] // 128) * 128
     bf16 = jnp.bfloat16
     dma = pltpu.SemaphoreType.DMA
@@ -457,9 +476,12 @@
     return pl.pallas_call(
         functools.partial(layer_kernel, (tok, width, n_z)),
         out_shape=jax.ShapeDtypeStruct((tok, half), bf16),
-        in_specs=[pl.BlockSpec(memory_space=vmem)] * 8,
+        in_specs=[pl.BlockSpec(memory_space=vmem)] * 10,
         out_specs=pl.BlockSpec(memory_space=vmem),
         scratch_shapes=[
+            vmem((tok, width + SPARE), bf16),
+            vmem(gate_up_scales.shape[1:], jnp.float32),
+            vmem((2 * down_scales.shape[1], lanes), jnp.float32),
             vmem((ep_count * tok, width + SPARE), bf16),
             vmem((width + SPARE, gate_up_codes.shape[2]), bf16),
             vmem((2, units, half), bf16),
@@ -491,14 +513,16 @@
             collective_id=0, has_side_effects=True, vmem_limit_bytes=63 * 1024 * 1024
         ),
     )(
-        payload,
-        own_cols,
+        hidden,
+        route_experts,
+        route_weight,
+        norm_gain.reshape(1, width),
         gate_up_codes[0],
-        gate_scales,
-        gate_up_bias.astype(jnp.float32),
+        gate_up_scales[0],
+        gate_up_bias,
         down_codes[0],
-        halves,
-        down_bias.astype(jnp.float32),
+        down_scales[0],
+        down_bias,
     )
 
 

time: 93.6 us -> 86.9 us (0.928)
  other arithmetic: 7.47 us -> 0 us
    convert_element_type x4 -> x0, other arithmetic: 4.43 us -> none  [the longest x1 1.3 us: dense_shards(): gate_up_bias.astype(jnp.float32)]
    unnamed x8 -> x4, local copies, waits for them, and re-layouts: 3.43 us -> 7.21 us
    reduce_sum x2 -> x0, other arithmetic: 1.92 us -> none  [the longest x1 1.21 us: rms_normed(): mean_square = jnp.mean(widened * widened, axis=-1, keepdims=True)]
    dynamic_slice x1 -> x0, local copies, waits for them, and re-layouts: 1.74 us -> none  [dense_shards(): own_cols = lax.dynamic_slice_in_dim(hidden, tp_rank * half, half, 1)]
    reshape x0 -> x1, local copies, waits for them, and re-layouts: none -> 1.29 us  [dense_shards(): norm_gain.reshape(1, width)]
    mul x2 -> x0, other arithmetic: 1.09 us -> none  [the longest x1 1.05 us: dense_shards(): gate_scales = gate_up_scales[0].astype(jnp.float32) * 0.5]
where the time goes in v2:
time: 86.9 us; the launch traced here: 86.7 us
  Pallas kernels  78.2 us (90%)
  local copies, waits for them, and re-layouts  8.51 us (10%)
    pallas_call x1, Pallas kernels, dense_shards(): pl.pallas_call(functools.partial(layer_kernel, (tok, width, n_z)), out_sh...  78.2 us
    unnamed x4, local copies, waits for them, and re-layouts  7.21 us

profile of v2, /device:TPU:0, one launch (start us, length us, event | category | flops | bytes accessed | tf_op | source)
XLA Modules:
  0.0 86.7 jit_solution(12421087605635957735)
XLA Ops:
  0.0 1.3 %reshape.3.gain = bf16[1,2880]{1,0:T(2,128)(2,1)} reshape(bf16[2880]{0:T(1024)(128)(2,1)} %param.13) | data formatting | bytes 11520 | tf_op jit(solution)/shard_map/reshape | solution.py:519
  1.3 1.4 %copy.12.routes = s32[64,4]{1,0:T(8,128)} copy(s32[64,4]{0,1:T(4,128)} %param.11) | data formatting | bytes 2048 | tf_op args[1]
  2.7 1.4 %copy.13.route_weights = f32[64,4]{1,0:T(8,128)} copy(f32[64,4]{0,1:T(4,128)} %param.12) | data formatting | bytes 2048 | tf_op args[2]
  4.0 2.8 %copy.11 = s32[1,1280,360]{2,1,0:T(8,128)} copy(s32[1,1280,360]{1,2,0:T(8,128)} %param.17) | data formatting | bytes 3686400 | tf_op args[7]
  6.9 78.2 %shard_map.100 = bf16[64,1440]{1,0:T(8,128)(2,1)} custom-call(bf16[64,2880]{1,0:T(8,128)(2,1)} %hidden.1, s32[64,4]{1,0:T(8,128)} %copy.12.routes, f32[64,4]{1,0:T(8,128)} %copy.13.route_weights, bf16[1,2880]{1,0:T(2,128)(2,1)} %reshape.3.gain, s32[360,2560]{1,0:T(8,128)} %bitcast.5, bf16[90,2560]{1,0:T(8,128)(2,1)} %bitcast.6, bf16[1,2560]{1,0:T(2,128)(2,1)} %gate_bias.1, ...), custom_call_target="tpu_custom_call" | custom-call | tf_op jit(solution)/shard_map/pallas_call | solution.py:476
  85.1 1.6 %copy.15 = bf16[64,1440]{1,0:T(8,128)(2,1)} copy(bf16[64,1440]{1,0:T(8,128)(2,1)} %shard_map.100) | data formatting | bytes 368640
